TPU v7x, 32 devices: a whole 2x2x4 slice. The times are simulated.
32 devices in a mesh: dp: 8 (over y, x, core), tensor: 4 (over z).
Axes of the slice: x: 2, y: 2, z: 4, core: 2. Of those that a mesh axis runs over, the one named last changes fastest.
Arguments:
- images: bfloat16 [8, 577, 1024], P('dp'), may hold values from -6 to 6
- valid_flags: int32 [8], P('dp'), may hold values from 0 to 1, as said below
- cotangent: bfloat16 [8, 577, 1024], P('dp'), may hold values from -6 to 6
- first_gain: float32 [1024], P('dp'), may hold values from 0.5 to 1.5
- first_shift: float32 [1024], P('dp'), may hold values from -1.75 to 1.75
- triple_weight: float32 [3, 1024, 1024], P(None, 'dp', 'tensor'), may hold values from -0.1875 to 0.1875
- pair_bias: float32 [2, 16, 64], P(None, 'tensor', 'dp'), may hold values from -1.75 to 1.75
- output_weight: float32 [1024, 1024], P('tensor', 'dp'), may hold values from -1.5 to 1.5
- output_bias: float32 [1024], P('dp'), may hold values from -1.75 to 1.75
- second_gain: float32 [1024], P('dp'), may hold values from 0.5 to 1.5
- second_shift: float32 [1024], P('dp'), may hold values from -1.75 to 1.75
- expand_weight: float32 [1024, 4096], P('dp', 'tensor'), may hold values from -1 to 1, as said below
- expand_bias: float32 [64, 64], P('tensor', 'dp'), may hold values from -1.75 to 1.75
- reduce_weight: float32 [4096, 1024], P('tensor', 'dp'), may hold values from -1 to 1, as said below
- reduce_bias: float32 [1024], P('dp'), may hold values from -1.75 to 1.75
- first_gain_mean: float32 [1024], P('dp'), may hold values from -6 to 6
- first_shift_mean: float32 [1024], P('dp'), may hold values from -6 to 6
- triple_weight_mean: float32 [3, 1024, 1024], P(None, 'dp', 'tensor'), may hold values from -6 to 6
- pair_bias_mean: float32 [2, 16, 64], P(None, 'tensor', 'dp'), may hold values from -6 to 6
- output_weight_mean: float32 [1024, 1024], P('tensor', 'dp'), may hold values from -6 to 6
- output_bias_mean: float32 [1024], P('dp'), may hold values from -6 to 6
- second_gain_mean: float32 [1024], P('dp'), may hold values from -6 to 6
- second_shift_mean: float32 [1024], P('dp'), may hold values from -6 to 6
- expand_weight_mean: float32 [1024, 4096], P('dp', 'tensor'), may hold values from -6 to 6
- expand_bias_mean: float32 [64, 64], P('tensor', 'dp'), may hold values from -6 to 6
- reduce_weight_mean: float32 [4096, 1024], P('tensor', 'dp'), may hold values from -6 to 6
- reduce_bias_mean: float32 [1024], P('dp'), may hold values from -6 to 6
- first_gain_square: float32 [1024], P('dp'), may hold values from 1 to 4
- first_shift_square: float32 [1024], P('dp'), may hold values from 1 to 4
- triple_weight_square: float32 [3, 1024, 1024], P(None, 'dp', 'tensor'), may hold values from 1 to 4
- pair_bias_square: float32 [2, 16, 64], P(None, 'tensor', 'dp'), may hold values from 1 to 4
- output_weight_square: float32 [1024, 1024], P('tensor', 'dp'), may hold values from 1 to 4
- output_bias_square: float32 [1024], P('dp'), may hold values from 1 to 4
- second_gain_square: float32 [1024], P('dp'), may hold values from 1 to 4
- second_shift_square: float32 [1024], P('dp'), may hold values from 1 to 4
- expand_weight_square: float32 [1024, 4096], P('dp', 'tensor'), may hold values from 1 to 4
- expand_bias_square: float32 [64, 64], P('tensor', 'dp'), may hold values from 1 to 4
- reduce_weight_square: float32 [4096, 1024], P('tensor', 'dp'), may hold values from 1 to 4
- reduce_bias_square: float32 [1024], P('dp'), may hold values from 1 to 4
Outputs:
- block_output: bfloat16 [8, 577, 1024], P('dp')
- input_grad: float32 [8, 577, 1024], P('dp')
- grad_norm: float32 [], replicated
- new_first_gain: float32 [1024], P('dp')
- mean_first_gain: float32 [1024], P('dp')
- square_first_gain: float32 [1024], P('dp')
- copy_first_gain: bfloat16 [1024], P('dp')
- new_first_shift: float32 [1024], P('dp')
- mean_first_shift: float32 [1024], P('dp')
- square_first_shift: float32 [1024], P('dp')
- copy_first_shift: bfloat16 [1024], P('dp')
- new_triple_weight: float32 [3, 1024, 1024], P(None, 'dp', 'tensor')
- mean_triple_weight: float32 [3, 1024, 1024], P(None, 'dp', 'tensor')
- square_triple_weight: float32 [3, 1024, 1024], P(None, 'dp', 'tensor')
- copy_triple_weight: bfloat16 [3, 1024, 1024], P(None, 'dp', 'tensor')
- new_pair_bias: float32 [2, 16, 64], P(None, 'tensor', 'dp')
- mean_pair_bias: float32 [2, 16, 64], P(None, 'tensor', 'dp')
- square_pair_bias: float32 [2, 16, 64], P(None, 'tensor', 'dp')
- copy_pair_bias: bfloat16 [2, 16, 64], P(None, 'tensor', 'dp')
- new_output_weight: float32 [1024, 1024], P('tensor', 'dp')
- mean_output_weight: float32 [1024, 1024], P('tensor', 'dp')
- square_output_weight: float32 [1024, 1024], P('tensor', 'dp')
- copy_output_weight: bfloat16 [1024, 1024], P('tensor', 'dp')
- new_output_bias: float32 [1024], P('dp')
- mean_output_bias: float32 [1024], P('dp')
- square_output_bias: float32 [1024], P('dp')
- copy_output_bias: bfloat16 [1024], P('dp')
- new_second_gain: float32 [1024], P('dp')
- mean_second_gain: float32 [1024], P('dp')
- square_second_gain: float32 [1024], P('dp')
- copy_second_gain: bfloat16 [1024], P('dp')
- new_second_shift: float32 [1024], P('dp')
- mean_second_shift: float32 [1024], P('dp')
- square_second_shift: float32 [1024], P('dp')
- copy_second_shift: bfloat16 [1024], P('dp')
- new_expand_weight: float32 [1024, 4096], P('dp', 'tensor')
- mean_expand_weight: float32 [1024, 4096], P('dp', 'tensor')
- square_expand_weight: float32 [1024, 4096], P('dp', 'tensor')
- copy_expand_weight: bfloat16 [1024, 4096], P('dp', 'tensor')
- new_expand_bias: float32 [64, 64], P('tensor', 'dp')
- mean_expand_bias: float32 [64, 64], P('tensor', 'dp')
- square_expand_bias: float32 [64, 64], P('tensor', 'dp')
- copy_expand_bias: bfloat16 [64, 64], P('tensor', 'dp')
- new_reduce_weight: float32 [4096, 1024], P('tensor', 'dp')
- mean_reduce_weight: float32 [4096, 1024], P('tensor', 'dp')
- square_reduce_weight: float32 [4096, 1024], P('tensor', 'dp')
- copy_reduce_weight: bfloat16 [4096, 1024], P('tensor', 'dp')
- new_reduce_bias: float32 [1024], P('dp')
- mean_reduce_bias: float32 [1024], P('dp')
- square_reduce_bias: float32 [1024], P('dp')
- copy_reduce_bias: bfloat16 [1024], P('dp')
Inputs may be any that keep to these rules, and one draw needn't show every extreme that they name: `valid_flags`: at least one image is blank; blank images may stand anywhere in the batch. `expand_weight`: a projection matrix with entries of order one over the root of 1024. `reduce_weight`: a projection matrix with entries of order one over the root of 4096.
All inputs are finite; a program needn't handle non-finite values.
Results may differ from a plain program's by a relative error of at most 0.012.
The roundings to bfloat16 on the way count: a program that leaves them out, or rounds other values in their place, can miss the bound.
Values may be sent and summed in bfloat16 or wider, within the bound.
A program may use at most 128 MiB of HBM per device.

v0:
```python
import math
import jax
import jax.numpy as jnp
from jax import lax
from jax.sharding import PartitionSpec as P

D = 1024
FF = 4096
shard_dims = (0, 0, 1, 2, 1, 0, 0, 0, 0, 1, 1, 0)
shared_terms = (1, 1, 0, 0, 0, 1, 1, 1, 0, 0, 0, 1)
rates = (0.2, 0.2, 0.03, 0.2, 0.03, 0.2, 0.2, 0.2, 0.03, 0.2, 0.03, 0.2)


def apply_layer_norm(input_row_block, norm_gain, norm_bias):
    center = jnp.mean(input_row_block, axis=-1, keepdims=True)
    centered_rows = input_row_block - center
    inverse_deviation = lax.rsqrt(
        jnp.mean(centered_rows * centered_rows, axis=-1, keepdims=True) + 1e-06
    )
    standardized_rows = centered_rows * inverse_deviation
    return (
        standardized_rows * norm_gain.astype(jnp.float32) + norm_bias.astype(jnp.float32),
        standardized_rows,
        inverse_deviation,
    )


def layer_norm_backward(incoming_gradient, standardized_rows, inverse_deviation, norm_gain):
    scaled_rows = incoming_gradient * norm_gain.astype(jnp.float32)
    return inverse_deviation * (
        scaled_rows
        - jnp.mean(scaled_rows, axis=-1, keepdims=True)
        - standardized_rows * jnp.mean(scaled_rows * standardized_rows, axis=-1, keepdims=True)
    )


def contract_rows(left, right):
    return lax.dot_general(
        left, right, (((0,), (0,)), ((), ())), preferred_element_type=jnp.float32
    )


def against(left, right):
    return lax.dot_general(
        left, right, (((1,), (1,)), ((), ())), preferred_element_type=jnp.float32
    )


def exact_gelu(values):
    return jax.nn.gelu(values, approximate=False)


def image_forward(parts):
    query, keys, values = parts
    factor = float(query.shape[2]) ** (-0.5)
    scores = jnp.einsum("qhd,khd->hqk", query, keys, preferred_element_type=jnp.float32) * factor
    top = jnp.max(scores, axis=-1, keepdims=True)
    totals = jnp.sum(jnp.exp(scores - top), axis=-1, keepdims=True)
    logsum = top + jnp.log(totals)
    probs = jnp.exp(scores - logsum).astype(jnp.bfloat16)
    mixed = jnp.einsum("hqk,khd->qhd", probs, values, preferred_element_type=jnp.float32)
    return (mixed.astype(jnp.bfloat16), logsum)


def image_backward(parts):
    query, keys, values, logsum, grad_mixed = parts
    factor = float(query.shape[2]) ** (-0.5)
    scores = jnp.einsum("qhd,khd->hqk", query, keys, preferred_element_type=jnp.float32) * factor
    probs = jnp.exp(scores - logsum)
    grad_probs = jnp.einsum("qhd,khd->hqk", grad_mixed, values, preferred_element_type=jnp.float32)
    grad_scores = probs * (grad_probs - jnp.sum(probs * grad_probs, axis=-1, keepdims=True))
    rounded = grad_scores.astype(jnp.bfloat16)
    grad_query = (
        jnp.einsum("hqk,khd->qhd", rounded, keys, preferred_element_type=jnp.float32) * factor
    )
    grad_keys = (
        jnp.einsum("hqk,qhd->khd", rounded, query, preferred_element_type=jnp.float32) * factor
    )
    grad_values = jnp.einsum(
        "hqk,qhd->khd", probs.astype(jnp.bfloat16), grad_mixed, preferred_element_type=jnp.float32
    )
    return (
        grad_query.astype(jnp.bfloat16),
        grad_keys.astype(jnp.bfloat16),
        grad_values.astype(jnp.bfloat16),
    )


def squared_total(grads, tensor_count):
    total = jnp.zeros((), jnp.float32)
    for incoming_gradient, shared in zip(grads, shared_terms):
        weight = 1.0 / tensor_count if shared else 1.0
        total = total + weight * jnp.sum(incoming_gradient * incoming_gradient)
    return total


def adam_step(master, row_mean, square, incoming_gradient, rate):
    mean_new = 0.5 * row_mean + 0.5 * incoming_gradient
    square_new = 0.5 * square + 0.5 * incoming_gradient * incoming_gradient
    change = -rate * (mean_new / (jnp.sqrt(square_new) + 1e-08) + 0.1 * master)
    updated = master + change
    return [updated, mean_new, square_new, updated.astype(jnp.bfloat16)]


def per_device(
    images,
    valid_flags,
    cotangent,
    first_gain,
    first_shift,
    triple_weight,
    pair_bias,
    output_weight,
    output_bias,
    second_gain,
    second_shift,
    expand_weight,
    expand_bias,
    reduce_weight,
    reduce_bias,
    first_gain_mean,
    first_shift_mean,
    triple_weight_mean,
    pair_bias_mean,
    output_weight_mean,
    output_bias_mean,
    second_gain_mean,
    second_shift_mean,
    expand_weight_mean,
    expand_bias_mean,
    reduce_weight_mean,
    reduce_bias_mean,
    first_gain_square,
    first_shift_square,
    triple_weight_square,
    pair_bias_square,
    output_weight_square,
    output_bias_square,
    second_gain_square,
    second_shift_square,
    expand_weight_square,
    expand_bias_square,
    reduce_weight_square,
    reduce_bias_square,
):
    masters = (
        first_gain,
        first_shift,
        triple_weight,
        pair_bias,
        output_weight,
        output_bias,
        second_gain,
        second_shift,
        expand_weight,
        expand_bias,
        reduce_weight,
        reduce_bias,
    )
    means = (
        first_gain_mean,
        first_shift_mean,
        triple_weight_mean,
        pair_bias_mean,
        output_weight_mean,
        output_bias_mean,
        second_gain_mean,
        second_shift_mean,
        expand_weight_mean,
        expand_bias_mean,
        reduce_weight_mean,
        reduce_bias_mean,
    )
    squares = (
        first_gain_square,
        first_shift_square,
        triple_weight_square,
        pair_bias_square,
        output_weight_square,
        output_bias_square,
        second_gain_square,
        second_shift_square,
        expand_weight_square,
        expand_bias_square,
        reduce_weight_square,
        reduce_bias_square,
    )
    rounded = tuple((master.astype(jnp.bfloat16) for master in masters))
    (
        first_norm_gain,
        first_norm_bias,
        triple,
        pairs,
        out_weight,
        out_bias,
        second_norm_gain,
        second_norm_bias,
        up_weight,
        up_bias,
        down_weight,
        down_bias,
    ) = (
        lax.all_gather(rounded[0], "dp", axis=0, tiled=True),
        lax.all_gather(rounded[1], "dp", axis=0, tiled=True),
        lax.all_gather(rounded[2], "dp", axis=1, tiled=True),
        lax.all_gather(rounded[3], "dp", axis=2, tiled=True),
        lax.all_gather(rounded[4], "dp", axis=1, tiled=True),
        lax.all_gather(rounded[5], "dp", axis=0, tiled=True),
        lax.all_gather(rounded[6], "dp", axis=0, tiled=True),
        lax.all_gather(rounded[7], "dp", axis=0, tiled=True),
        lax.all_gather(rounded[8], "dp", axis=0, tiled=True),
        lax.all_gather(rounded[9], "dp", axis=1, tiled=True),
        lax.all_gather(rounded[10], "dp", axis=1, tiled=True),
        lax.all_gather(rounded[11], "dp", axis=0, tiled=True),
    )
    shape = images.shape
    count = shape[0] * shape[1]
    heads_local = pairs.shape[1]
    head_size = pairs.shape[2]
    split = (shape[0], shape[1], heads_local, head_size)
    tensor_count = lax.axis_size("tensor")
    input_row_block = images.reshape(count, shape[2]).astype(jnp.float32)
    first_normed_rows, first_standardized, first_inverse_deviation = apply_layer_norm(
        input_row_block, first_norm_gain, first_norm_bias
    )
    inputs_one = first_normed_rows.astype(jnp.bfloat16)
    projected = jnp.einsum("td,cde->cte", inputs_one, triple, preferred_element_type=jnp.float32)
    pair_flat = pairs.reshape(2, -1).astype(jnp.float32)
    query = (projected[0] + pair_flat[0]).astype(jnp.bfloat16).reshape(split)
    keys = projected[1].astype(jnp.bfloat16).reshape(split)
    values = (projected[2] + pair_flat[1]).astype(jnp.bfloat16).reshape(split)
    mixed, logsum = lax.map(image_forward, (query, keys, values))
    mixed_flat = mixed.reshape(count, -1)
    attn_part = jnp.dot(mixed_flat, out_weight, preferred_element_type=jnp.float32)
    middle_state = input_row_block + lax.psum(attn_part, "tensor") + out_bias.astype(jnp.float32)
    second_normed_rows, second_standardized, second_inverse_deviation = apply_layer_norm(
        middle_state, second_norm_gain, second_norm_bias
    )
    inputs_two = second_normed_rows.astype(jnp.bfloat16)
    hidden = jnp.dot(inputs_two, up_weight, preferred_element_type=jnp.float32) + up_bias.reshape(
        -1
    ).astype(jnp.float32)
    active_full, gelu_back = jax.vjp(exact_gelu, hidden)
    active = active_full.astype(jnp.bfloat16)
    mlp_part = jnp.dot(active, down_weight, preferred_element_type=jnp.float32)
    result = middle_state + lax.psum(mlp_part, "tensor") + down_bias.astype(jnp.float32)
    block_output = result.astype(jnp.bfloat16)
    output_gradient = (
        cotangent.astype(jnp.float32) * valid_flags.astype(jnp.float32)[:, None, None]
    ).reshape(count, -1)
    grad_low = output_gradient.astype(jnp.bfloat16)
    grad_down_bias = jnp.sum(output_gradient, axis=0)
    grad_down_weight = contract_rows(active, grad_low)
    grad_active = against(grad_low, down_weight)
    grad_hidden = gelu_back(grad_active)[0]
    grad_up_bias = jnp.sum(grad_hidden, axis=0).reshape(up_bias.shape)
    hidden_low = grad_hidden.astype(jnp.bfloat16)
    grad_up_weight = contract_rows(inputs_two, hidden_low)
    second_normed_gradient = lax.psum(against(hidden_low, up_weight), "tensor")
    second_gain_gradient = jnp.sum(second_normed_gradient * second_standardized, axis=0)
    grad_shift_two = jnp.sum(second_normed_gradient, axis=0)
    middle_gradient = output_gradient + layer_norm_backward(
        second_normed_gradient, second_standardized, second_inverse_deviation, second_norm_gain
    )
    grad_out_bias = jnp.sum(middle_gradient, axis=0)
    middle_low = middle_gradient.astype(jnp.bfloat16)
    grad_out_weight = contract_rows(mixed_flat, middle_low)
    grad_mixed = against(middle_low, out_weight).astype(jnp.bfloat16).reshape(split)
    grad_query, grad_keys, grad_values = lax.map(
        image_backward, (query, keys, values, logsum, grad_mixed)
    )
    stacked = jnp.stack(
        [
            grad_query.reshape(count, -1),
            grad_keys.reshape(count, -1),
            grad_values.reshape(count, -1),
        ]
    )
    grad_pairs = jnp.stack(
        [
            jnp.sum(stacked[0].astype(jnp.float32), axis=0),
            jnp.sum(stacked[2].astype(jnp.float32), axis=0),
        ]
    ).reshape(pairs.shape)
    grad_triple = jnp.einsum("td,cte->cde", inputs_one, stacked, preferred_element_type=jnp.float32)
    back_one = jnp.einsum("cte,cde->td", stacked, triple, preferred_element_type=jnp.float32)
    first_normed_gradient = lax.psum(back_one, "tensor")
    first_gain_gradient = jnp.sum(first_normed_gradient * first_standardized, axis=0)
    grad_shift_one = jnp.sum(first_normed_gradient, axis=0)
    row_gradient = middle_gradient + layer_norm_backward(
        first_normed_gradient, first_standardized, first_inverse_deviation, first_norm_gain
    )
    grads = (
        first_gain_gradient,
        grad_shift_one,
        grad_triple,
        grad_pairs,
        grad_out_weight,
        grad_out_bias,
        second_gain_gradient,
        grad_shift_two,
        grad_up_weight,
        grad_up_bias,
        grad_down_weight,
        grad_down_bias,
    )
    summed = lax.psum(
        (
            grads[0],
            grads[1],
            grads[2],
            grads[3],
            grads[4],
            grads[5],
            grads[6],
            grads[7],
            grads[8],
            grads[9],
            grads[10],
            grads[11],
        ),
        "dp",
    )
    total = lax.psum(squared_total(summed, tensor_count), "tensor")
    position = lax.axis_index("dp")
    owned = tuple(
        (
            lax.dynamic_slice_in_dim(
                incoming_gradient, position * master.shape[dim], master.shape[dim], dim
            )
            for incoming_gradient, master, dim in zip(summed, masters, shard_dims)
        )
    )
    norm_value = jnp.sqrt(total)
    limit = math.sqrt(4 * D * D + 2 * D * FF + 8 * D + FF)
    factor = jnp.minimum(1.0, limit / (norm_value + 1e-06))
    updates = []
    for master, row_mean, square, incoming_gradient, rate in zip(
        masters, means, squares, owned, rates
    ):
        updates.extend(adam_step(master, row_mean, square, incoming_gradient * factor, rate))
    return (block_output.reshape(shape), row_gradient.reshape(shape), norm_value, *updates)


def solution(mesh):
    in_specs = (
        P("dp", None, None),
        P("dp"),
        P("dp", None, None),
        P("dp"),
        P("dp"),
        P(None, "dp", "tensor"),
        P(None, "tensor", "dp"),
        P("tensor", "dp"),
        P("dp"),
        P("dp"),
        P("dp"),
        P("dp", "tensor"),
        P("tensor", "dp"),
        P("tensor", "dp"),
        P("dp"),
        P("dp"),
        P("dp"),
        P(None, "dp", "tensor"),
        P(None, "tensor", "dp"),
        P("tensor", "dp"),
        P("dp"),
        P("dp"),
        P("dp"),
        P("dp", "tensor"),
        P("tensor", "dp"),
        P("tensor", "dp"),
        P("dp"),
        P("dp"),
        P("dp"),
        P(None, "dp", "tensor"),
        P(None, "tensor", "dp"),
        P("tensor", "dp"),
        P("dp"),
        P("dp"),
        P("dp"),
        P("dp", "tensor"),
        P("tensor", "dp"),
        P("tensor", "dp"),
        P("dp"),
    )
    out_specs = (
        P("dp", None, None),
        P("dp", None, None),
        P(),
        P("dp"),
        P("dp"),
        P("dp"),
        P("dp"),
        P("dp"),
        P("dp"),
        P("dp"),
        P("dp"),
        P(None, "dp", "tensor"),
        P(None, "dp", "tensor"),
        P(None, "dp", "tensor"),
        P(None, "dp", "tensor"),
        P(None, "tensor", "dp"),
        P(None, "tensor", "dp"),
        P(None, "tensor", "dp"),
        P(None, "tensor", "dp"),
        P("tensor", "dp"),
        P("tensor", "dp"),
        P("tensor", "dp"),
        P("tensor", "dp"),
        P("dp"),
        P("dp"),
        P("dp"),
        P("dp"),
        P("dp"),
        P("dp"),
        P("dp"),
        P("dp"),
        P("dp"),
        P("dp"),
        P("dp"),
        P("dp"),
        P("dp", "tensor"),
        P("dp", "tensor"),
        P("dp", "tensor"),
        P("dp", "tensor"),
        P("tensor", "dp"),
        P("tensor", "dp"),
        P("tensor", "dp"),
        P("tensor", "dp"),
        P("tensor", "dp"),
        P("tensor", "dp"),
        P("tensor", "dp"),
        P("tensor", "dp"),
        P("dp"),
        P("dp"),
        P("dp"),
        P("dp"),
    )
    return jax.shard_map(
        per_device, mesh=mesh, in_specs=in_specs, out_specs=out_specs, check_vma=False
    )
```

profile of v0, /device:TPU:0, one launch (start us, length us, event | category | flops | bytes accessed | tf_op | source)
XLA Modules:
  0.0 777.6 jit_solution(4180550084816320558)
XLA Ops:
  7.3 1.8 convert_element_type.208
  9.8 10.3 %all-gather.1 = bf16[8,1,128]{2,1,0:T(2,128)(2,1)S(1)} all-gather(bf16[1,1,128]{2,1,0:T(2,128)(2,1)S(1)} %convert_bitcast_fusion.5), channel_id=1, replica_groups=mesh['dp'=8,'tensor'=4] {'dp'}, dimensions={0}, use_global_device_ids=true | all-gather | bytes 2304 | tf_op jit(solution)/shard_map/all_gather | solution.py:204
  20.7 8.8 %all-gather = bf16[8,1,128]{2,1,0:T(2,128)(2,1)S(1)} all-gather(bf16[1,1,128]{2,1,0:T(2,128)(2,1)S(1)} %convert_bitcast_fusion.6), channel_id=1, replica_groups=mesh['dp'=8,'tensor'=4] {'dp'}, dimensions={0}, use_global_device_ids=true | all-gather | bytes 2304 | tf_op jit(solution)/shard_map/all_gather | solution.py:203
  30.3 8.1 %all_gather.39 = bf16[2,4,64]{1,0,2:T(2,128)(2,1)S(1)} all-gather(bf16[2,4,8]{1,0,2:T(2,128)(2,1)S(1)} %copy.199), channel_id=1, replica_groups=mesh['dp'=8,'tensor'=4] {'dp'}, dimensions={2}, use_global_device_ids=true | all-gather | bytes 1152 | tf_op jit(solution)/shard_map/all_gather | solution.py:206
  39.5 10.1 %all_gather.40 = bf16[256,1024]{1,0:T(8,128)(2,1)S(1)} all-gather(bf16[256,128]{1,0:T(8,128)(2,1)S(1)} %convert_element_type.217), channel_id=1, replica_groups=mesh['dp'=8,'tensor'=4] {'dp'}, dimensions={1}, use_global_device_ids=true | all-gather | bytes 589824 | tf_op jit(solution)/shard_map/all_gather | solution.py:207
  50.4 2.8 convolution_bitcast_fusion.2
  53.8 1.2 multiply_reduce_fusion.1
  55.0 1.0 exponential_reduce_fusion
  56.1 1.5 copy-done
  57.8 3.9 convolution_convert_fusion.1
  61.8 2.0 fusion.93
  65.6 7.8 %all-gather.2 = bf16[8,1,128]{2,1,0:T(2,128)(2,1)S(1)} all-gather(bf16[1,1,128]{2,1,0:T(2,128)(2,1)S(1)} %convert_bitcast_fusion.4), channel_id=1, replica_groups=mesh['dp'=8,'tensor'=4] {'dp'}, dimensions={0}, use_global_device_ids=true | all-gather | bytes 2304 | tf_op jit(solution)/shard_map/all_gather | solution.py:208
  73.5 8.9 %all_gather.45 = bf16[16,64]{0,1:T(8,128)(2,1)S(1)} all-gather(bf16[16,8]{0,1:T(8,128)(2,1)S(1)} %convert_element_type.226), channel_id=1, replica_groups=mesh['dp'=8,'tensor'=4] {'dp'}, dimensions={1}, use_global_device_ids=true | all-gather | bytes 2304 | tf_op jit(solution)/shard_map/all_gather | solution.py:212
  82.5 7.8 %all-gather.4 = bf16[8,1,128]{2,1,0:T(2,128)(2,1)S(1)} all-gather(bf16[1,1,128]{2,1,0:T(2,128)(2,1)S(1)} %convert_bitcast_fusion.2), channel_id=1, replica_groups=mesh['dp'=8,'tensor'=4] {'dp'}, dimensions={0}, use_global_device_ids=true | all-gather | bytes 2304 | tf_op jit(solution)/shard_map/all_gather | solution.py:210
  90.3 9.2 %all-gather.3 = bf16[8,1,128]{2,1,0:T(2,128)(2,1)S(1)} all-gather(bf16[1,1,128]{2,1,0:T(2,128)(2,1)S(1)} %convert_bitcast_fusion.3), channel_id=1, replica_groups=mesh['dp'=8,'tensor'=4] {'dp'}, dimensions={0}, use_global_device_ids=true | all-gather | bytes 2304 | tf_op jit(solution)/shard_map/all_gather | solution.py:209
  100.2 59.8 %all-reduce.8.cloned.1.call-done = f32[577,1024]{1,0:T(8,128)} async-done(((f32[577,1024]{1,0:T(8,128)}), f32[577,1024]{1,0:T(8,128)}) %all-reduce.8.cloned.1.call-update) | async-done | bytes 2363408 | tf_op jit(solution)/shard_map/psum | solution.py:235
  160.0 2.4 fusion.88
  162.8 26.4 %all-gather.12.cloned.1.call-done = bf16[1024,1024]{1,0:T(8,128)(2,1)} async-done(((bf16[128,1024]{1,0:T(8,128)(2,1)}), bf16[1024,1024]{1,0:T(8,128)(2,1)}) %all-gather.12.cloned.1.call-update) | async-done | bytes 2097168 | tf_op jit(solution)/shard_map/all_gather | solution.py:211
  189.2 10.2 %multiply_convert_fusion.1 = (bf16[577,1024]{1,0:T(8,128)(2,1)}, f32[577,1024]{1,0:T(8,128)}, f32[577,1024]{1,0:T(8,128)}) fusion(f32[1024]{0:T(1024)S(1)} %reshape.236, bf16[1024,1024]{1,0:T(8,128)(2,1)} %all-gather.12.cloned.1.call-done, f32[577,1024]{1,0:T(8,128)S(1)} %get-tuple-element.426, f32[1024]{0:T(1024)S(1)} %bitcast.159, ...), kind=kOutput, calls=%fused_computation.39 | convolution fusion | flops 1252006912 | bytes 10385928 | tf_op jit(solution)/shard_map/dot_general | solution.py:240
  199.4 20.3 %all-gather.14.cloned.1.call-done = bf16[1024,1024]{1,0:T(8,128)(2,1)} async-done(((bf16[1024,128]{1,0:T(8,128)(2,1)}), bf16[1024,1024]{1,0:T(8,128)(2,1)}) %all-gather.14.cloned.1.call-update) | async-done | bytes 2097168 | tf_op jit(solution)/shard_map/all_gather | solution.py:213
  219.7 5.7 fusion.92
  225.4 1.0 copy-done.55
  226.4 2.9 fusion.37
  229.6 4.9 fusion.94
  234.5 90.8 %all-reduce.10.cloned.1.call-done = f32[577,1024]{1,0:T(8,128)} async-done(((f32[577,1024]{1,0:T(8,128)}), f32[577,1024]{1,0:T(8,128)}) %all-reduce.10.cloned.1.call-update) | async-done | bytes 2363408 | tf_op jit(solution)/shard_map/psum | solution.py:259
  325.3 2.8 multiply_reduce_fusion.5
  329.1 1.5 copy-done.1
  330.6 1.2 convolution_convert_fusion.2
  331.9 1.9 copy.206
  333.7 4.8 convert_reduce_fusion.1
  338.6 4.4 multiply_reduce_fusion
  343.0 1.4 multiply_convert_fusion
  344.5 1.7 fusion.27
  346.2 1.4 convert_reduce_fusion.2
  347.8 1.1 copy.211
  348.9 1.8 copy.210
  350.7 4.0 convolution_bitcast_fusion.1
  355.1 5.7 fusion.30
  360.8 4.1 fusion.35
  364.9 1.6 fusion.32
  366.5 3.5 convolution_bitcast_fusion
  371.1 1.2 copy.215
  372.3 1.9 copy.214
  374.2 1.6 fusion.20
  375.9 152.1 %all-reduce.14.cloned.1.call-done = (f32[577,1024]{1,0:T(8,128)}, f32[577,1024]{1,0:T(8,128)}) async-done(((f32[577,1024]{1,0:T(8,128)}, f32[577,1024]{1,0:T(8,128)}), (f32[577,1024]{1,0:T(8,128)}, f32[577,1024]{1,0:T(8,128)})) %all-reduce.14.cloned.1.call-update) | async-done | bytes 4726800 | tf_op jit(solution)/shard_map/psum | solution.py:246
  528.0 3.0 fusion.16
  531.1 26.5 %all-reduce = (f32[1024]{0:T(1024)S(1)}, f32[1024]{0:T(1024)S(1)}, f32[2,4,64]{2,1,0:T(4,128)S(1)}, f32[1024]{0:T(1024)S(1)}, f32[1024]{0:T(1024)S(1)}, /*index=...) all-reduce(f32[1024]{0:T(1024)S(1)} %get-tuple-element.353, ...), channel_id=1, replica_groups=mesh['dp'=8,'tensor'=4] {'dp'}, use_global_device_ids=true, to_apply=%region_16.17 | all-reduce | flops 7680 | bytes 61440 | tf_op jit(solution)/shard_map/psum | solution.py:307
  566.4 5.5 fusion.15
  571.8 132.6 %all-reduce.12.cloned.1.call-done = (f32[3,1024,256]{1,2,0:T(8,128)}, f32[256,1024]{1,0:T(8,128)}, f32[1024,1024]{1,0:T(8,128)}, f32[1024,1024]{1,0:T(8,128)}) async-done(((f32[3,1024,256]{1,2,0:T(8,128)}, f32[256,1024]{1,0:T(8,128)}, f32[1024,1024]{1,0:T(8,128)}, f32[1024,1024]{1,0:T(8,128)}), (f32[3,1024,256]{1,2,0:T(8,128)}, f32[256,1024]{1,0:T(8,128)}, f32[1024,1024]{1,0:T(8,128)}, ...) | async-done | bytes 12582928 | tf_op jit(solution)/shard_map/psum | solution.py:307
  704.5 3.5 multiply_reduce_fusion.4
  707.9 2.2 multiply_reduce_fusion.10
  710.2 1.7 multiply_reduce_fusion.3
  711.9 1.7 multiply_reduce_fusion.2
  717.5 5.5 copy.218
  723.0 12.2 %psum.135 = f32[]{:T(128)} all-reduce(f32[]{:T(128)S(6)} %add.421), channel_id=1, replica_groups=mesh['dp'=8,'tensor'=4] {'tensor'}, use_global_device_ids=true, to_apply=%region_48.49 | all-reduce | flops 1 | bytes 8 | tf_op jit(solution)/shard_map/psum | solution.py:324
  736.5 8.7 %all-gather.5 = bf16[8,1,128]{2,1,0:T(2,128)(2,1)S(1)} all-gather(bf16[1,1,128]{2,1,0:T(2,128)(2,1)S(1)} %get-tuple-element.431), channel_id=1, replica_groups=mesh['dp'=8,'tensor'=4] {'dp'}, dimensions={0}, use_global_device_ids=true | all-gather | bytes 2304 | tf_op jit(solution)/shard_map/all_gather | solution.py:214
  745.3 2.3 fusion.80
  747.6 1.9 copy.219
  749.5 1.9 copy.220
  751.4 1.9 copy.221
  754.3 3.5 fusion.28
  759.2 1.8 fusion.76
  762.9 2.6 fusion.68
  766.8 2.6 fusion.64
  (192 shorter events, 21.1 us)
Async XLA Ops:
  7.2 42.4 %copy-start.3 = (bf16[1,577,1024]{2,1,0:T(8,128)(2,1)S(1)}, bf16[1,577,1024]{2,1,0:T(8,128)(2,1)}, u32[]{:S(2)}) copy-start(bf16[1,577,1024]{2,1,0:T(8,128)(2,1)} %param.39) | copy-start | bytes 3545092
  7.3 43.2 %all-gather.10.cloned.1.call-start = ((), (), s32[]{:S(2)}) async-start(), calls=%async_computation | async-start | bytes 1769472 | tf_op jit(solution)/shard_map/all_gather | solution.py:205
  9.1 150.9 %all-reduce.8.cloned.1.call-start = ((), (), s32[]{:S(2)}) async-start(), calls=%async_computation.1 | async-start | bytes 4784128 | tf_op jit(solution)/shard_map/psum | solution.py:235
  49.7 12.1 %copy-start.11 = (bf16[256,1024]{1,0:T(8,128)(2,1)}, bf16[256,1024]{1,0:T(8,128)(2,1)S(1)}, u32[]{:S(2)}) copy-start(bf16[256,1024]{1,0:T(8,128)(2,1)S(1)} %all_gather.40) | copy-start | bytes 1572868
  53.6 1.5 copy-start.14
  53.8 1.2 copy-start.6
  55.0 2.5 copy-start
  61.8 2.1 copy-start.16
  63.8 1.0 copy-start.18
  63.8 1.8 copy-start.42
  63.8 9.7 %copy-start.31 = (f32[16,8]{0,1:T(8,128)S(1)}, f32[16,8]{0,1:T(8,128)}, u32[]{:S(2)}) copy-start(f32[16,8]{0,1:T(8,128)} %param.51) | copy-start | bytes 1540
  63.8 18.7 %copy-start.48 = (f32[128]{0:T(128)S(1)}, f32[128]{0:T(128)}, u32[]{:S(2)}) copy-start(f32[128]{0:T(128)} %param.49) | copy-start | bytes 1540
  63.8 26.6 %copy-start.45 = (f32[128]{0:T(128)S(1)}, f32[128]{0:T(128)}, u32[]{:S(2)}) copy-start(f32[128]{0:T(128)} %param.48) | copy-start | bytes 1540
  63.8 125.4 %all-gather.12.cloned.1.call-start = ((), (), s32[]{:S(2)}) async-start(), calls=%async_computation.2 | async-start | bytes 2359296 | tf_op jit(solution)/shard_map/all_gather | solution.py:211
  64.6 155.1 %all-gather.14.cloned.1.call-start = ((), (), s32[]{:S(2)}) async-start(), calls=%async_computation.3 | async-start | bytes 2359296 | tf_op jit(solution)/shard_map/all_gather | solution.py:213
  65.6 259.8 %all-reduce.10.cloned.1.call-start = ((), (), s32[]{:S(2)}) async-start(), calls=%async_computation.4 | async-start | bytes 4784128 | tf_op jit(solution)/shard_map/psum | solution.py:259
  219.7 6.8 copy-start.54
  229.4 298.7 %all-reduce.14.cloned.1.call-start = ((), (), s32[]{:S(2)}) async-start(), calls=%async_computation.6 | async-start | bytes 9568256 | tf_op jit(solution)/shard_map/psum | solution.py:246
  325.3 2.8 copy-start.5
  325.3 2.8 copy-start.10
  328.1 2.5 copy-start.12
  329.1 1.5 copy-start.1
  333.7 4.8 copy-start.13
  333.7 9.3 %slice-start = ((s8[5980160]{0:T(1024)(128)(4,1)}), s8[4194304]{0:T(1024)(128)(4,1)S(1)}, s32[]{:S(2)}) async-start(s8[5980160]{0:T(1024)(128)(4,1)} %bitcast.128), calls=%async_computation.7 | async-start | bytes 8388608
  338.6 4.4 slice-start.1
  343.0 1.4 copy-start.7
  344.5 1.7 copy-start.15
  346.2 1.4 copy-start.21
  354.8 349.7 %all-reduce.12.cloned.1.call-start = ((), (), s32[]{:S(2)}) async-start(), calls=%async_computation.5 | async-start | bytes 25165824 | tf_op jit(solution)/shard_map/psum | solution.py:307
  355.1 5.7 copy-start.56
  360.8 4.1 copy-start.2
  364.9 1.6 copy-start.4
  364.9 1.6 copy-start.27
  704.5 5.7 copy-start.9
  707.9 3.9 copy-start.8
  713.5 22.4 %copy-start.51 = (f32[128]{0:T(128)S(1)}, f32[128]{0:T(128)}, u32[]{:S(2)}) copy-start(f32[128]{0:T(128)} %param.53) | copy-start | bytes 1540
  713.5 22.4 %copy-start.52 = (f32[128]{0:T(128)S(1)}, f32[128]{0:T(128)}, u32[]{:S(2)}) copy-start(f32[128]{0:T(128)} %param.77) | copy-start | bytes 1540
  713.5 22.4 %copy-start.53 = (f32[128]{0:T(128)S(1)}, f32[128]{0:T(128)}, u32[]{:S(2)}) copy-start(f32[128]{0:T(128)} %param.65) | copy-start | bytes 1540
  754.2 3.7 copy-start.36
  754.2 3.7 copy-start.37
  754.2 3.7 copy-start.38
  754.2 4.3 copy-start.39
  754.2 4.3 copy-start.40
  754.2 4.3 copy-start.41
  754.2 4.9 copy-start.26
  754.2 4.9 copy-start.28
  754.2 4.9 copy-start.29
  754.2 6.8 copy-start.43
  754.2 6.8 copy-start.44
  754.2 7.4 copy-start.46
  754.3 7.4 copy-start.47
  754.3 8.0 %copy-start.49 = (f32[128]{0:T(128)S(1)}, f32[128]{0:T(128)}, u32[]{:S(2)}) copy-start(f32[128]{0:T(128)} %param.73) | copy-start | bytes 1540
  754.3 8.0 %copy-start.50 = (f32[128]{0:T(128)S(1)}, f32[128]{0:T(128)}, u32[]{:S(2)}) copy-start(f32[128]{0:T(128)} %param.61) | copy-start | bytes 1540
  754.3 8.6 %copy-start.17 = (f32[128,1024]{1,0:T(8,128)S(1)}, f32[128,1024]{1,0:T(8,128)}, u32[]{:S(2)}) copy-start(f32[128,1024]{1,0:T(8,128)} %param.50) | copy-start | bytes 1572868
  754.3 8.6 %copy-start.22 = (f32[128,1024]{1,0:T(8,128)S(1)}, f32[128,1024]{1,0:T(8,128)}, u32[]{:S(2)}) copy-start(f32[128,1024]{1,0:T(8,128)} %param.74) | copy-start | bytes 1572868
  754.3 8.6 %copy-start.23 = (f32[128,1024]{1,0:T(8,128)S(1)}, f32[128,1024]{1,0:T(8,128)}, u32[]{:S(2)}) copy-start(f32[128,1024]{1,0:T(8,128)} %param.62) | copy-start | bytes 1572868
  759.1 6.4 copy-start.30
  759.1 6.4 copy-start.32
  759.1 6.3 copy-start.33
  759.1 7.0 copy-start.34
  759.2 7.0 copy-start.35
  759.2 7.6 copy-start.19
  759.2 7.6 copy-start.24
  759.2 7.6 copy-start.25
  (2 other events, 2.0 us)
Sparse Core Ops, SparseCore 0:
  10.5 28.3 all-gather.9
  63.9 96.0 all-reduce.7
  162.5 26.7 all-gather.11
  191.5 28.0 all-gather.13
  229.5 95.7 all-reduce.9
  354.9 173.0 all-reduce.13
  532.6 171.8 all-reduce.11
where the time goes:
time: 785 us; the launch traced here: 778 us
  waiting for transfers between devices  482 us (61%)
  blocking collectives  118 us (15%)
  matrix products  66.1 us (8%)
  other arithmetic  57.7 us (7%)
  local copies, waits for them, and re-layouts  27 us (3%)
  between operations  25.5 us (3%)
    psum x1, waiting for transfers between devices, per_device(): lax.psum(mlp_part, 'tensor')  152 us
    psum x1, waiting for transfers between devices, per_device(): lax.psum((grads[0], grads[1], grads[2], grads[3], grads[4], grads[5], gra...  133 us
    psum x1, waiting for transfers between devices, per_device(): second_normed_gradient = lax.psum(against(hidden_low, up_weight), 'tensor')  90.8 us
    psum x1, waiting for transfers between devices, per_device(): lax.psum(attn_part, 'tensor')  59.8 us
    psum x1, blocking collectives, per_device(): lax.psum((grads[0], grads[1], grads[2], grads[3], grads[4], grads[5], gra...  26.5 us
    all_gather x1, waiting for transfers between devices, per_device(): lax.all_gather(rounded[8], 'dp', axis=0, tiled=True)  26.4 us
    unnamed x126, local copies, waits for them, and re-layouts  20.7 us
    all_gather x1, waiting for transfers between devices, per_device(): lax.all_gather(rounded[10], 'dp', axis=1, tiled=True)  20.3 us
  transfers between devices with their start and end apart: 7, of which 6 were waited for; matrix products, arithmetic and copies ran while one was open for 7% of the time, Pallas kernels for 0%

commit v1 on v0

--- a/solution.py
+++ b/solution.py
@@ -243,7 +243,11 @@
     active_full, gelu_back = jax.vjp(exact_gelu, hidden)
     active = active_full.astype(jnp.bfloat16)
     mlp_part = jnp.dot(active, down_weight, preferred_element_type=jnp.float32)
-    result = middle_state + lax.psum(mlp_part, "tensor") + down_bias.astype(jnp.float32)
+    result = (
+        middle_state
+        + jnp.sum(lax.all_gather(mlp_part, "tensor"), axis=0)
+        + down_bias.astype(jnp.float32)
+    )
     block_output = result.astype(jnp.bfloat16)
     output_gradient = (
         cotangent.astype(jnp.float32) * valid_flags.astype(jnp.float32)[:, None, None]

time: 785 us -> 864 us (1.10)
  waiting for transfers between devices: 482 us -> 561 us
    all_gather x0 -> x1, waiting for transfers between devices: none -> 167 us  [per_device(): lax.all_gather(mlp_part, 'tensor')]
    psum x1, waiting for transfers between devices: 152 us -> 73.1 us  [per_device(): first_normed_gradient = lax.psum(back_one, 'tensor')]
    psum x1, waiting for transfers between devices: 90.8 us -> 81.5 us  [per_device(): second_normed_gradient = lax.psum(against(hidden_low, up_weight), 'tensor')]
    unnamed x126 -> x124, local copies, waits for them, and re-layouts: 20.7 us -> 15.3 us
  transfers between devices with their start and end apart: 7 -> 8, of which waited for: 6 -> 7; matrix products, arithmetic and copies ran while one was open for 7% -> 7% of each run, Pallas kernels for 0% -> 0%
where the time goes in v1:
time: 864 us; the launch traced here: 856 us
  waiting for transfers between devices  561 us (65%)
  blocking collectives  119 us (14%)
  matrix products  65.8 us (8%)
  other arithmetic  62.9 us (7%)
  between operations  25.5 us (3%)
  local copies, waits for them, and re-layouts  21.6 us (2%)
    all_gather x1, waiting for transfers between devices, per_device(): lax.all_gather(mlp_part, 'tensor')  167 us
    psum x1, waiting for transfers between devices, per_device(): lax.psum((grads[0], grads[1], grads[2], grads[3], grads[4], grads[5], gra...  133 us
    psum x1, waiting for transfers between devices, per_device(): second_normed_gradient = lax.psum(against(hidden_low, up_weight), 'tensor')  81.5 us
    psum x1, waiting for transfers between devices, per_device(): first_normed_gradient = lax.psum(back_one, 'tensor')  73.1 us
    psum x1, waiting for transfers between devices, per_device(): lax.psum(attn_part, 'tensor')  59.8 us
    psum x1, blocking collectives, per_device(): lax.psum((grads[0], grads[1], grads[2], grads[3], grads[4], grads[5], gra...  26.5 us
    all_gather x1, waiting for transfers between devices, per_device(): lax.all_gather(rounded[8], 'dp', axis=0, tiled=True)  26.4 us
    all_gather x1, waiting for transfers between devices, per_device(): lax.all_gather(rounded[10], 'dp', axis=1, tiled=True)  20.3 us
  transfers between devices with their start and end apart: 8, of which 7 were waited for; matrix products, arithmetic and copies ran while one was open for 7% of the time, Pallas kernels for 0%

profile of v1, /device:TPU:0, one launch (start us, length us, event | category | flops | bytes accessed | tf_op | source)
XLA Modules:
  0.0 856.3 jit_solution(12178948492963406852)
XLA Ops:
  7.3 1.8 convert_element_type.208
  9.8 10.3 %all-gather.2 = bf16[8,1,128]{2,1,0:T(2,128)(2,1)S(1)} all-gather(bf16[1,1,128]{2,1,0:T(2,128)(2,1)S(1)} %convert_bitcast_fusion.5), channel_id=1, replica_groups=mesh['dp'=8,'tensor'=4] {'dp'}, dimensions={0}, use_global_device_ids=true | all-gather | bytes 2304 | tf_op jit(solution)/shard_map/all_gather | solution.py:204
  20.7 8.8 %all-gather.1 = bf16[8,1,128]{2,1,0:T(2,128)(2,1)S(1)} all-gather(bf16[1,1,128]{2,1,0:T(2,128)(2,1)S(1)} %convert_bitcast_fusion.6), channel_id=1, replica_groups=mesh['dp'=8,'tensor'=4] {'dp'}, dimensions={0}, use_global_device_ids=true | all-gather | bytes 2304 | tf_op jit(solution)/shard_map/all_gather | solution.py:203
  30.3 8.1 all_gather.45
  38.6 0.9 convert_element_type.217
  39.5 10.1 %all_gather.46 = bf16[256,1024]{1,0:T(8,128)(2,1)S(1)} all-gather(bf16[256,128]{1,0:T(8,128)(2,1)S(1)} %convert_element_type.217), channel_id=1, replica_groups=mesh['dp'=8,'tensor'=4] {'dp'}, dimensions={1}, use_global_device_ids=true | all-gather | bytes 589824 | tf_op jit(solution)/shard_map/all_gather | solution.py:207
  50.4 2.8 convolution_bitcast_fusion.3
  53.8 1.2 multiply_reduce_fusion.1
  55.0 1.0 exponential_reduce_fusion
  56.1 1.6 copy-done
  57.9 3.9 convolution_convert_fusion.1
  61.8 1.9 fusion.93
  65.6 7.9 all_gather.51
  73.7 8.8 %all-gather.3 = bf16[8,1,128]{2,1,0:T(2,128)(2,1)S(1)} all-gather(bf16[1,1,128]{2,1,0:T(2,128)(2,1)S(1)} %convert_bitcast_fusion.4), channel_id=1, replica_groups=mesh['dp'=8,'tensor'=4] {'dp'}, dimensions={0}, use_global_device_ids=true | all-gather | bytes 2304 | tf_op jit(solution)/shard_map/all_gather | solution.py:208
  82.5 7.8 all-gather.5
  90.3 9.2 %all-gather.4 = bf16[8,1,128]{2,1,0:T(2,128)(2,1)S(1)} all-gather(bf16[1,1,128]{2,1,0:T(2,128)(2,1)S(1)} %convert_bitcast_fusion.3), channel_id=1, replica_groups=mesh['dp'=8,'tensor'=4] {'dp'}, dimensions={0}, use_global_device_ids=true | all-gather | bytes 2304 | tf_op jit(solution)/shard_map/all_gather | solution.py:209
  100.2 59.8 %all-reduce.7.cloned.1.call-done = f32[577,1024]{1,0:T(8,128)} async-done(((f32[577,1024]{1,0:T(8,128)}), f32[577,1024]{1,0:T(8,128)}) %all-reduce.7.cloned.1.call-update) | async-done | bytes 2363408 | tf_op jit(solution)/shard_map/psum | solution.py:235
  160.0 2.4 fusion.88
  162.8 26.4 %all-gather.15.cloned.1.call-done = bf16[1024,1024]{1,0:T(8,128)(2,1)} async-done(((bf16[128,1024]{1,0:T(8,128)(2,1)}), bf16[1024,1024]{1,0:T(8,128)(2,1)}) %all-gather.15.cloned.1.call-update) | async-done | bytes 2097168 | tf_op jit(solution)/shard_map/all_gather | solution.py:211
  189.3 10.2 %multiply_convert_fusion.1 = (bf16[577,1024]{1,0:T(8,128)(2,1)}, f32[577,1024]{1,0:T(8,128)}, f32[577,1024]{1,0:T(8,128)}) fusion(f32[1024]{0:T(1024)S(1)} %reshape.236, bf16[1024,1024]{1,0:T(8,128)(2,1)} %all-gather.15.cloned.1.call-done, f32[577,1024]{1,0:T(8,128)S(1)} %get-tuple-element.424, f32[1024]{0:T(1024)S(1)} %bitcast.161, ...), kind=kOutput, calls=%fused_computation.39 | convolution fusion | flops 1252006912 | bytes 10385928 | tf_op jit(solution)/shard_map/dot_general | solution.py:240
  199.4 20.3 %all-gather.17.cloned.1.call-done = bf16[1024,1024]{1,0:T(8,128)(2,1)} async-done(((bf16[1024,128]{1,0:T(8,128)(2,1)}), bf16[1024,1024]{1,0:T(8,128)(2,1)}) %all-gather.17.cloned.1.call-update) | async-done | bytes 2097168 | tf_op jit(solution)/shard_map/all_gather | solution.py:213
  219.7 5.7 fusion.92
  225.4 1.1 copy-done.54
  226.5 2.9 fusion.37
  229.5 4.8 convolution_bitcast_fusion.2
  235.0 8.9 %all-gather.7 = bf16[8,1,128]{2,1,0:T(2,128)(2,1)S(1)} all-gather(bf16[1,1,128]{2,1,0:T(2,128)(2,1)S(1)} %convert_bitcast_fusion.1), channel_id=1, replica_groups=mesh['dp'=8,'tensor'=4] {'dp'}, dimensions={0}, use_global_device_ids=true | all-gather | bytes 2304 | tf_op jit(solution)/shard_map/all_gather | solution.py:214
  243.9 81.5 %all-reduce.9.cloned.1.call-done = f32[577,1024]{1,0:T(8,128)} async-done(((f32[577,1024]{1,0:T(8,128)}), f32[577,1024]{1,0:T(8,128)}) %all-reduce.9.cloned.1.call-update) | async-done | bytes 2363408 | tf_op jit(solution)/shard_map/psum | solution.py:263
  325.4 2.6 multiply_reduce_fusion.5
  328.0 166.7 %all-gather.19.cloned.1.call-done = f32[4,577,1024]{2,1,0:T(8,128)} async-done(((f32[1,577,1024]{2,1,0:T(8,128)}), f32[4,577,1024]{2,1,0:T(8,128)}) %all-gather.19.cloned.1.call-update) | async-done | bytes 9453584 | tf_op jit(solution)/shard_map/all_gather | solution.py:248
  494.7 6.5 reduce_sum.295
  501.2 4.9 fusion.86
  506.2 1.3 convolution_convert_fusion.2
  507.4 1.9 copy.206
  509.3 4.8 convert_reduce_fusion.1
  514.1 4.4 multiply_reduce_fusion
  518.6 1.4 multiply_convert_fusion
  520.0 1.7 fusion.27
  521.7 1.4 convert_reduce_fusion.2
  523.3 1.1 copy.211
  524.4 1.8 copy.210
  526.3 4.1 convolution_bitcast_fusion.1
  530.7 5.6 fusion.30
  536.3 4.1 fusion.35
  540.4 1.6 fusion.32
  541.9 3.5 convolution_bitcast_fusion
  545.4 1.0 copy-done.19
  546.6 1.2 copy.215
  547.7 1.9 copy.214
  549.7 1.6 fusion.20
  551.4 73.1 %all-reduce.11.cloned.1.call-done = f32[577,1024]{1,0:T(8,128)} async-done(((f32[577,1024]{1,0:T(8,128)}), f32[577,1024]{1,0:T(8,128)}) %all-reduce.11.cloned.1.call-update) | async-done | bytes 2363408 | tf_op jit(solution)/shard_map/psum | solution.py:291
  624.5 3.0 fusion.16
  627.6 26.5 %all-reduce = (f32[1024]{0:T(1024)S(1)}, f32[1024]{0:T(1024)S(1)}, f32[2,4,64]{2,1,0:T(4,128)S(1)}, f32[1024]{0:T(1024)S(1)}, f32[1024]{0:T(1024)S(1)}, /*index=...) all-reduce(f32[1024]{0:T(1024)S(1)} %get-tuple-element.353, ...), channel_id=1, replica_groups=mesh['dp'=8,'tensor'=4] {'dp'}, use_global_device_ids=true, to_apply=%region_16.17 | all-reduce | flops 7680 | bytes 61440 | tf_op jit(solution)/shard_map/psum | solution.py:311
  662.8 4.8 fusion.15
  667.6 133.4 %all-reduce.13.cloned.1.call-done = (f32[3,1024,256]{1,2,0:T(8,128)}, f32[256,1024]{1,0:T(8,128)}, f32[1024,1024]{1,0:T(8,128)}, f32[1024,1024]{1,0:T(8,128)}) async-done(((f32[3,1024,256]{1,2,0:T(8,128)}, f32[256,1024]{1,0:T(8,128)}, f32[1024,1024]{1,0:T(8,128)}, f32[1024,1024]{1,0:T(8,128)}), (f32[3,1024,256]{1,2,0:T(8,128)}, f32[256,1024]{1,0:T(8,128)}, f32[1024,1024]{1,0:T(8,128)}, ...) | async-done | bytes 12582928 | tf_op jit(solution)/shard_map/psum | solution.py:311
  801.0 3.5 multiply_reduce_fusion.4
  804.4 2.2 multiply_reduce_fusion.10
  806.7 1.7 multiply_reduce_fusion.3
  808.3 1.7 multiply_reduce_fusion.2
  813.9 3.8 copy.218
  817.8 12.2 %psum.127 = f32[]{:T(128)} all-reduce(f32[]{:T(128)S(6)} %add.419), channel_id=1, replica_groups=mesh['dp'=8,'tensor'=4] {'tensor'}, use_global_device_ids=true, to_apply=%region_48.49 | all-reduce | flops 1 | bytes 8 | tf_op jit(solution)/shard_map/psum | solution.py:328
  830.8 1.5 fusion.80
  837.3 1.8 fusion.76
  841.0 2.5 fusion.68
  844.9 2.5 fusion.64
  (194 shorter events, 21.4 us)
Async XLA Ops:
  7.2 42.4 %copy-start.3 = (bf16[1,577,1024]{2,1,0:T(8,128)(2,1)S(1)}, bf16[1,577,1024]{2,1,0:T(8,128)(2,1)}, u32[]{:S(2)}) copy-start(bf16[1,577,1024]{2,1,0:T(8,128)(2,1)} %param.39) | copy-start | bytes 3545092
  7.3 43.2 %all-gather.13.cloned.1.call-start = ((), (), s32[]{:S(2)}) async-start(), calls=%async_computation | async-start | bytes 1769472 | tf_op jit(solution)/shard_map/all_gather | solution.py:205
  9.1 150.9 %all-reduce.7.cloned.1.call-start = ((), (), s32[]{:S(2)}) async-start(), calls=%async_computation.1 | async-start | bytes 4784128 | tf_op jit(solution)/shard_map/psum | solution.py:235
  49.7 12.2 %copy-start.10 = (bf16[256,1024]{1,0:T(8,128)(2,1)}, bf16[256,1024]{1,0:T(8,128)(2,1)S(1)}, u32[]{:S(2)}) copy-start(bf16[256,1024]{1,0:T(8,128)(2,1)S(1)} %all_gather.46) | copy-start | bytes 1572868
  53.6 1.4 copy-start.13
  53.8 1.2 copy-start.6
  55.0 2.6 copy-start
  61.8 2.0 copy-start.15
  63.8 1.0 copy-start.17
  63.8 1.8 copy-start.30
  63.8 10.0 %copy-start.41 = (f32[128]{0:T(128)S(1)}, f32[128]{0:T(128)}, u32[]{:S(2)}) copy-start(f32[128]{0:T(128)} %param.47) | copy-start | bytes 1540
  63.8 18.7 %copy-start.47 = (f32[128]{0:T(128)S(1)}, f32[128]{0:T(128)}, u32[]{:S(2)}) copy-start(f32[128]{0:T(128)} %param.49) | copy-start | bytes 1540
  63.8 26.6 %copy-start.44 = (f32[128]{0:T(128)S(1)}, f32[128]{0:T(128)}, u32[]{:S(2)}) copy-start(f32[128]{0:T(128)} %param.48) | copy-start | bytes 1540
  63.8 125.4 %all-gather.15.cloned.1.call-start = ((), (), s32[]{:S(2)}) async-start(), calls=%async_computation.2 | async-start | bytes 2359296 | tf_op jit(solution)/shard_map/all_gather | solution.py:211
  64.6 155.1 %all-gather.17.cloned.1.call-start = ((), (), s32[]{:S(2)}) async-start(), calls=%async_computation.3 | async-start | bytes 2359296 | tf_op jit(solution)/shard_map/all_gather | solution.py:213
  65.6 259.8 %all-reduce.9.cloned.1.call-start = ((), (), s32[]{:S(2)}) async-start(), calls=%async_computation.4 | async-start | bytes 4784128 | tf_op jit(solution)/shard_map/psum | solution.py:263
  162.4 163.0 %copy-start.1 = (f32[577,1024]{1,0:T(8,128)}, f32[577,1024]{1,0:T(8,128)S(1)}, u32[]{:S(2)}) copy-start(f32[577,1024]{1,0:T(8,128)S(1)} %get-tuple-element.424) | copy-start | bytes 7090180
  219.7 6.9 copy-start.53
  225.4 1.1 copy-start.54
  229.4 265.2 %all-gather.19.cloned.1.call-start = ((), (), s32[]{:S(2)}) async-start(), calls=%async_computation.6 | async-start | bytes 11960320 | tf_op jit(solution)/shard_map/all_gather | solution.py:248
  234.3 390.2 %all-reduce.11.cloned.1.call-start = ((), (), s32[]{:S(2)}) async-start(), calls=%async_computation.5 | async-start | bytes 4784128 | tf_op jit(solution)/shard_map/psum | solution.py:291
  501.2 4.9 copy-start.11
  509.3 4.8 copy-start.12
  509.3 9.3 %slice-start = ((s8[5980160]{0:T(1024)(128)(4,1)}), s8[4194304]{0:T(1024)(128)(4,1)S(1)}, s32[]{:S(2)}) async-start(s8[5980160]{0:T(1024)(128)(4,1)} %bitcast.130), calls=%async_computation.8 | async-start | bytes 8388608
  514.1 4.4 slice-start.1
  518.6 1.4 copy-start.7
  520.0 1.7 copy-start.14
  521.7 1.4 copy-start.20
  530.4 270.5 %all-reduce.13.cloned.1.call-start = ((), (), s32[]{:S(2)}) async-start(), calls=%async_computation.7 | async-start | bytes 25165824 | tf_op jit(solution)/shard_map/psum | solution.py:311
  530.7 5.6 copy-start.2
  530.7 5.6 copy-start.55
  540.4 1.6 copy-start.4
  540.4 1.6 copy-start.26
  801.0 5.7 copy-start.9
  804.4 3.9 copy-start.8
  808.3 5.6 copy-start.5
  830.7 5.3 copy-start.35
  830.7 5.3 copy-start.36
  830.7 5.3 copy-start.37
  830.7 5.9 copy-start.38
  830.7 5.9 copy-start.39
  830.7 5.8 copy-start.40
  830.8 6.5 copy-start.25
  830.8 6.4 copy-start.27
  832.3 4.9 copy-start.28
  832.3 6.9 copy-start.42
  832.3 6.9 copy-start.43
  832.3 7.5 copy-start.45
  832.3 7.5 copy-start.46
  832.3 8.1 copy-start.48
  832.3 8.1 copy-start.49
  832.4 8.7 %copy-start.16 = (f32[128,1024]{1,0:T(8,128)S(1)}, f32[128,1024]{1,0:T(8,128)}, u32[]{:S(2)}) copy-start(f32[128,1024]{1,0:T(8,128)} %param.50) | copy-start | bytes 1572868
  832.4 8.6 %copy-start.21 = (f32[128,1024]{1,0:T(8,128)S(1)}, f32[128,1024]{1,0:T(8,128)}, u32[]{:S(2)}) copy-start(f32[128,1024]{1,0:T(8,128)} %param.74) | copy-start | bytes 1572868
  832.4 8.6 %copy-start.22 = (f32[128,1024]{1,0:T(8,128)S(1)}, f32[128,1024]{1,0:T(8,128)}, u32[]{:S(2)}) copy-start(f32[128,1024]{1,0:T(8,128)} %param.62) | copy-start | bytes 1572868
  837.2 6.3 copy-start.29
  837.2 6.3 copy-start.31
  837.2 6.3 copy-start.32
  837.3 7.0 copy-start.33
  837.3 7.0 copy-start.34
  837.3 7.6 copy-start.18
  837.3 7.6 copy-start.23
  837.3 7.6 copy-start.24
  843.6 3.9 copy-start.51
  843.6 3.9 copy-start.52
  (2 other events, 1.7 us)
Sparse Core Ops, SparseCore 0:
  10.5 28.3 all-gather.12
  63.9 96.0 all-reduce.6
  162.5 26.7 all-gather.14
  191.6 28.0 all-gather.16
  229.6 95.7 all-reduce.8
  326.8 167.8 all-gather.18
  530.5 93.9 all-reduce.10
  629.1 171.8 all-reduce.12
